TPU v7x, 256 devices: a whole 4x4x8 slice. The times are simulated.
256 devices in a mesh: gz: 64 (over z, x, core), col: 4 (over y).
Axes of the slice: x: 4, y: 4, z: 8, core: 2. Of those that a mesh axis runs over, the one named last changes fastest.
Arguments:
- source: float32 [4096, 2048], P('gz', 'col'), may hold values from -6 to 6
- z_vectors: float32 [4096, 4096], P('gz', 'col'), may hold values from -0.25 to 0.25
- x_vectors: float32 [4, 4], replicated, may hold values from -3 to 3
- y_vectors: float32 [512, 512], replicated, may hold values from -0.25 to 0.25
- z_values: float32 [4096], replicated, may hold values from 0.1 to 3
- x_values: float32 [4], replicated, may hold values from 0.1 to 3
- y_values: float32 [512], replicated, may hold values from 0.1 to 3
Outputs:
- solution: float32 [4096, 2048], P('gz', 'col')
All inputs are finite; a program needn't handle non-finite values.
Results may differ from a plain program's by a relative error of at most 0.000092.
Values sent between devices are 32-bit elements; how exact they have to be, the bound alone decides.
A program may use at most 64 MiB of HBM per device.

v0:
```python
import jax
import jax.numpy as jnp
from jax import lax
from jax.sharding import Mesh
from jax.sharding import PartitionSpec as P

GZ = ("gz_0", "gz_1", "gz_2")
exact_mode = lax.Precision.HIGHEST


def in_order(pieces, dim):
    shape = list(pieces.shape[1:])
    shape[dim] *= pieces.shape[0]
    return jnp.moveaxis(pieces, 0, dim).reshape(shape)


def sent_to_all(value, axis):
    devices = lax.axis_size(axis)
    return lax.all_to_all(
        jnp.broadcast_to(value[None], (devices, *value.shape)), axis, 0, 0, tiled=True
    )


def gather_directly(value, axis, dim):
    return in_order(sent_to_all(value, axis), dim)


def own_rows(subtotal, axes):
    for axis in axes:
        subtotal = lax.psum_scatter(subtotal, axis, scatter_dimension=0, tiled=True)
    return subtotal


def cut_along(value, dim, devices):
    shape = value.shape
    pieces = value.reshape(*shape[:dim], devices, shape[dim] // devices, *shape[dim + 1 :])
    return jnp.moveaxis(pieces, dim, 0)


def sum_at_owner(value, axis, dim):
    devices = lax.axis_size(axis)
    pieces = lax.all_to_all(cut_along(value, dim, devices), axis, 0, 0, tiled=True)
    return jnp.sum(pieces, axis=0)


def lead_product(left_side, right_side):
    return lax.dot_general(
        left_side,
        right_side,
        (((0,), (0,)), ((), ())),
        precision=exact_mode,
        preferred_element_type=jnp.float32,
    )


def shards(source, z_vectors, x_vectors, y_vectors, z_values, x_values, y_values):
    z_rows = source.shape[0]
    width_y = y_vectors.shape[0]
    width_x = x_vectors.shape[0]
    x_lines = source.shape[1] // width_y
    column = lax.axis_index("col")
    row_block = lax.axis_index(GZ)
    along_y = jnp.dot(source, y_vectors, precision=exact_mode, preferred_element_type=jnp.float32)
    planes = gather_directly(along_y, "col", 1)
    modal_full = jnp.einsum(
        "zxj,xi->zij", planes.reshape(z_rows, width_x, width_y), x_vectors, precision=exact_mode
    )
    modal_full = modal_full.reshape(z_rows, width_x * width_y)
    part_rows = z_rows // lax.axis_size("col")
    coeffs = own_rows(lead_product(z_vectors, modal_full), GZ)
    mode_start = column * z_vectors.shape[1] + row_block * part_rows
    z_part = lax.dynamic_slice_in_dim(z_values, mode_start, part_rows, 0)
    divisor = z_part[:, None, None] + x_values[None, :, None] + y_values[None, None, :]
    scaled = (coeffs.reshape(part_rows, width_x, width_y) / divisor).reshape(
        part_rows, width_x * width_y
    )
    back_z = jnp.dot(
        z_vectors,
        lax.all_gather(scaled, GZ, axis=0, tiled=True),
        precision=exact_mode,
        preferred_element_type=jnp.float32,
    )
    spread_x = jnp.einsum(
        "zij,xi->zxj", back_z.reshape(z_rows, width_x, width_y), x_vectors, precision=exact_mode
    )
    summed = sum_at_owner(spread_x.reshape(z_rows, width_x * width_y), "col", 1)
    back_x = summed.reshape(z_rows, x_lines, width_y)
    solution = lax.dot_general(
        back_x.reshape(z_rows * x_lines, width_y),
        y_vectors,
        (((1,), (1,)), ((), ())),
        precision=exact_mode,
        preferred_element_type=jnp.float32,
    )
    return solution


def solution(mesh):
    torus = Mesh(mesh.devices.reshape(8, 4, 2, mesh.shape["col"]), ("gz_0", "gz_1", "gz_2", "col"))
    return jax.shard_map(
        shards,
        mesh=torus,
        in_specs=(P(GZ, "col"), P(GZ, "col"), P(), P(), P(), P(), P()),
        out_specs=P(GZ, "col"),
        check_vma=False,
    )
```

profile of v0, /device:TPU:1, one launch (start us, length us, event | category | flops | bytes accessed | tf_op | source)
XLA Modules:
  0.0 293.1 jit_solution(16918401710747406262)
XLA Ops:
  6.5 1.2 copy-done
  7.8 1.7 fusion.7
  9.4 0.1 broadcast_in_dim.2
  9.5 13.4 %all_to_all.10 = f32[4,64,512]{2,1,0:T(8,128)S(1)} all-to-all(f32[4,64,512]{2,1,0:T(8,128)S(1)} %broadcast_in_dim.2), channel_id=1, replica_groups=mesh['gz_0'=8,'gz_1'=4,'gz_2'=2,'col'=4] {'col'}, dimensions={0} | all-to-all | bytes 1048576 | tf_op jit(solution)/shard_map/all_to_all | solution.py:19
  22.9 2.0 fusion.1
  24.9 0.2 copy.19
  25.1 10.0 %convolution_bitcast_fusion = f32[1024,2048]{0,1:T(8,128)} fusion(f32[64,2048]{1,0:T(8,128)S(1)} %bitcast.37, f32[64,1024]{1,0:T(8,128)} %param.8), kind=kOutput, calls=%fused_computation | convolution fusion | flops 1610612736 | bytes 9175040 | tf_op jit(solution)/shard_map/dot_general | solution.py:47
  35.1 0.0 reduce-scatter.10.cloned.1.call-start
  35.2 97.1 %reduce-scatter.8.cloned.1.call-done = f32[128,2048]{0,1:T(8,128)} async-done(((f32[1024,2048]{0,1:T(8,128)}), f32[128,2048]{0,1:T(8,128)}) %reduce-scatter.8.cloned.1.call-update) | async-done | bytes 1048592 | tf_op jit(solution)/shard_map/reduce_scatter | solution.py:30
  132.2 2.5 copy.15
  134.8 23.6 %reduce-scatter.10.cloned.1.call-done = f32[32,2048]{1,0:T(8,128)} async-done(((f32[128,2048]{1,0:T(8,128)}), f32[32,2048]{1,0:T(8,128)}) %reduce-scatter.10.cloned.1.call-update) | async-done | bytes 262160
  158.6 0.8 dynamic_slice.3
  159.3 0.1 broadcast_add_fusion
  159.4 16.6 %reduce-scatter.12.cloned.1.call-done = f32[16,2048]{1,0:T(8,128)} async-done(((f32[32,2048]{1,0:T(8,128)}), f32[16,2048]{1,0:T(8,128)}) %reduce-scatter.12.cloned.1.call-update) | async-done | bytes 131088
  176.0 1.2 copy.18
  177.2 0.3 fusion
  177.6 1.0 copy.11
  178.6 84.0 %all-gather.2.cloned.1.call-done = f32[1024,2048]{1,0:T(8,128)} async-done(((f32[16,2048]{1,0:T(8,128)}), f32[1024,2048]{1,0:T(8,128)}) %all-gather.2.cloned.1.call-update) | async-done | bytes 8388624 | tf_op jit(solution)/shard_map/all_gather | solution.py:79
  262.6 7.8 %convolution_bitcast_fusion.1 = f32[64,2048]{1,0:T(8,128)S(1)} fusion(f32[1024,2048]{1,0:T(8,128)} %all-gather.2.cloned.1.call-done, f32[64,1024]{1,0:T(8,128)S(1)} %copy-done.1), kind=kOutput, calls=%fused_computation.1 | convolution fusion | flops 1610612736 | bytes 9175040 | tf_op jit(solution)/shard_map/dot_general | solution.py:77
  270.4 0.4 reshape.45
  270.7 1.0 fusion.4
  271.8 0.2 copy.26
  271.9 12.8 %all_to_all.11 = f32[4,64,512]{2,1,0:T(8,128)S(1)} all-to-all(f32[4,64,512]{2,1,0:T(8,128)S(1)} %bitcast.39), channel_id=1, replica_groups=mesh['gz_0'=8,'gz_1'=4,'gz_2'=2,'col'=4] {'col'}, dimensions={0} | all-to-all | bytes 1048576 | tf_op jit(solution)/shard_map/all_to_all | solution.py:42
  284.8 1.8 fusion.8
  (19 shorter events, 0.2 us)
Async XLA Ops:
  6.5 1.2 copy-start
  6.5 125.7 %reduce-scatter.8.cloned.1.call-start = ((), (), s32[]{:S(2)}) async-start(), calls=%async_computation.5 | async-start | bytes 9437184 | tf_op jit(solution)/shard_map/reduce_scatter | solution.py:30
  35.1 123.4 %copy-start.3 = (f32[512]{0:T(512)S(1)}, f32[512]{0:T(512)}, u32[]{:S(2)}) copy-start(f32[512]{0:T(512)} %param.13) | copy-start | bytes 6148
  35.1 124.2 %copy-start.4 = (f32[4]{0:T(128)S(1)}, f32[4]{0:T(128)}, u32[]{:S(2)}) copy-start(f32[4]{0:T(128)} %param.12) | copy-start | bytes 52
  35.1 227.5 %copy-start.1 = (f32[64,1024]{1,0:T(8,128)S(1)}, f32[64,1024]{1,0:T(8,128)}, u32[]{:S(2)}) copy-start(f32[64,1024]{1,0:T(8,128)} %param.8) | copy-start | bytes 786436
  35.1 123.3 %reduce-scatter.10.cloned.1.call-start = ((), (), s32[]{:S(2)}) async-start(), calls=%async_computation.7 | async-start | bytes 1310720
  134.8 136.0 %copy-start.2 = (f32[4,4]{1,0:T(4,128)S(1)}, f32[4,4]{1,0:T(4,128)}, u32[]{:S(2)}) copy-start(f32[4,4]{1,0:T(4,128)} %param.9) | copy-start | bytes 196
  134.8 41.2 %reduce-scatter.12.cloned.1.call-start = ((), (), s32[]{:S(2)}) async-start(), calls=%async_computation.8 | async-start | bytes 393216
  158.5 104.1 %all-gather.2.cloned.1.call-start = ((), (), s32[]{:S(2)}) async-start(), calls=%async_computation.6 | async-start | bytes 8519680 | tf_op jit(solution)/shard_map/all_gather | solution.py:79
Sparse Core Ops, SparseCore 0:
  35.3 96.9 reduce-scatter.7
  134.9 23.4 reduce-scatter.9
  160.9 14.9 reduce-scatter.11
  178.7 83.8 all-gather.1
where the time goes:
time: 293 us
  waiting for transfers between devices  221 us (75%)
  blocking collectives  26.3 us (9%)
  matrix products  24.3 us (8%)
  between operations  13.3 us (5%)
  local copies, waits for them, and re-layouts  7.47 us (3%)
    reduce_scatter x1, waiting for transfers between devices, own_rows(): subtotal = lax.psum_scatter(subtotal, axis, scatter_dimension=0, tiled=True)  97.1 us
    all_gather x1, waiting for transfers between devices, shards(): lax.all_gather(scaled, GZ, axis=0, tiled=True)  84 us
    unnamed x6, waiting for transfers between devices  40.2 us
    all_to_all x1, blocking collectives, sent_to_all(): lax.all_to_all(jnp.broadcast_to(value[None], (devices, *value.shape)), ax...  13.4 us
    all_to_all x1, blocking collectives, sum_at_owner(): lax.all_to_all(cut_along(value, dim, devices), axis, 0, 0, tiled=True)  12.8 us
    dot_general x1, matrix products, lead_product(): lax.dot_general(left_side, right_side, (((0,), (0,)), ((), ())), precisio...  10 us
    dot_general x1, matrix products, shards(): jnp.dot(z_vectors, lax.all_gather(scaled, GZ, axis=0, tiled=True), precis...  7.81 us
  transfers between devices with their start and end apart: 4, of which 4 were waited for; matrix products, arithmetic and copies ran while one was open for 0% of the time, Pallas kernels for 0%

commit v1 on v0

--- a/solution.py
+++ b/solution.py
@@ -76,7 +76,7 @@
     )
     back_z = jnp.dot(
         z_vectors,
-        lax.all_gather(scaled, GZ, axis=0, tiled=True),
+        jnp.concatenate(lax.all_to_all(jnp.stack([scaled] * lax.axis_size(GZ)), GZ, 0, 0), axis=0),
         precision=exact_mode,
         preferred_element_type=jnp.float32,
     )

time: 293 us -> 402 us (1.37)
  blocking collectives: 26.3 us -> 219 us
  waiting for transfers between devices: 221 us -> 137 us
    all_to_all x0 -> x1, blocking collectives: none -> 194 us  [shards(): lax.all_to_all(jnp.stack([scaled] * lax.axis_size(GZ)), GZ, 0, 0)]
    all_gather x1 -> x0, waiting for transfers between devices: 84 us -> none  [shards(): lax.all_gather(scaled, GZ, axis=0, tiled=True)]
    unnamed x6 -> x5, waiting for transfers between devices: 40.2 us -> 40.3 us
  transfers between devices with their start and end apart: 4 -> 3, of which waited for: 4 -> 3; matrix products, arithmetic and copies ran while one was open for 0% -> 0% of each run, Pallas kernels for 0% -> 0%
where the time goes in v1:
time: 402 us; the launch traced here: 399 us
  blocking collectives  219 us (54%)
  waiting for transfers between devices  137 us (34%)
  matrix products  21.9 us (5%)
  between operations  13.2 us (3%)
  local copies, waits for them, and re-layouts  7.85 us (2%)
    all_to_all x1, blocking collectives, shards(): lax.all_to_all(jnp.stack([scaled] * lax.axis_size(GZ)), GZ, 0, 0)  194 us
    reduce_scatter x1, waiting for transfers between devices, own_rows(): subtotal = lax.psum_scatter(subtotal, axis, scatter_dimension=0, tiled=True)  97.1 us
    unnamed x5, waiting for transfers between devices  40.3 us
    all_to_all x1, blocking collectives, sent_to_all(): lax.all_to_all(jnp.broadcast_to(value[None], (devices, *value.shape)), ax...  13.4 us
    all_to_all x1, blocking collectives, sum_at_owner(): lax.all_to_all(cut_along(value, dim, devices), axis, 0, 0, tiled=True)  10.7 us
    dot_general x1, matrix products, lead_product(): lax.dot_general(left_side, right_side, (((0,), (0,)), ((), ())), precisio...  9.94 us
  transfers between devices with their start and end apart: 3, of which 3 were waited for; matrix products, arithmetic and copies ran while one was open for 0% of the time, Pallas kernels for 0%

profile of v1, /device:TPU:1, one launch (start us, length us, event | category | flops | bytes accessed | tf_op | source)
XLA Modules:
  0.0 399.4 jit_solution(13178243082120037823)
XLA Ops:
  6.5 1.2 copy-done
  7.8 1.7 fusion.7
  9.4 0.1 broadcast_in_dim.2
  9.5 13.4 %all_to_all.15 = f32[4,64,512]{2,1,0:T(8,128)S(1)} all-to-all(f32[4,64,512]{2,1,0:T(8,128)S(1)} %broadcast_in_dim.2), channel_id=1, replica_groups=mesh['gz_0'=8,'gz_1'=4,'gz_2'=2,'col'=4] {'col'}, dimensions={0} | all-to-all | bytes 1048576 | tf_op jit(solution)/shard_map/all_to_all | solution.py:19
  22.9 2.0 fusion.1
  24.9 0.2 copy.20
  25.1 9.9 %convolution_bitcast_fusion = f32[1024,2048]{0,1:T(8,128)} fusion(f32[64,2048]{1,0:T(8,128)S(1)} %bitcast.39, f32[64,1024]{1,0:T(8,128)} %param.8), kind=kOutput, calls=%fused_computation | convolution fusion | flops 1610612736 | bytes 9175040 | tf_op jit(solution)/shard_map/dot_general | solution.py:47
  35.1 97.1 %reduce-scatter.8.cloned.1.call-done = f32[128,2048]{0,1:T(8,128)} async-done(((f32[1024,2048]{0,1:T(8,128)}), f32[128,2048]{0,1:T(8,128)}) %reduce-scatter.8.cloned.1.call-update) | async-done | bytes 1048592 | tf_op jit(solution)/shard_map/reduce_scatter | solution.py:30
  132.1 2.5 copy.16
  134.8 23.6 %reduce-scatter.10.cloned.1.call-done = f32[32,2048]{1,0:T(8,128)} async-done(((f32[128,2048]{1,0:T(8,128)}), f32[32,2048]{1,0:T(8,128)}) %reduce-scatter.10.cloned.1.call-update) | async-done | bytes 262160
  158.4 0.8 dynamic_slice.3
  159.1 0.1 broadcast_add_fusion
  159.2 16.7 %reduce-scatter.12.cloned.1.call-done = f32[16,2048]{1,0:T(8,128)} async-done(((f32[32,2048]{1,0:T(8,128)}), f32[16,2048]{1,0:T(8,128)}) %reduce-scatter.12.cloned.1.call-update) | async-done | bytes 131088
  175.9 1.2 copy.19
  177.1 0.3 fusion
  177.5 0.3 copy.12
  177.8 1.0 stack.3
  178.8 194.4 %all_to_all.16 = f32[64,16,2048]{2,1,0:T(8,128)S(1)} all-to-all(f32[64,16,2048]{2,1,0:T(8,128)S(1)} %stack.3), channel_id=1, replica_groups=mesh['gz_0'=8,'gz_1'=4,'gz_2'=2,'col'=4] {'gz_0','gz_1','gz_2'}, dimensions={0} | all-to-all | bytes 16777216 | tf_op jit(solution)/shard_map/all_to_all | solution.py:79
  373.2 5.6 %convolution_bitcast_fusion.1 = f32[64,2048]{1,0:T(8,128)S(1)} fusion(f32[1024,2048]{1,0:T(8,128)S(1)} %bitcast.38, f32[64,1024]{1,0:T(8,128)S(1)} %copy-done.1), kind=kOutput, calls=%fused_computation.1 | convolution fusion | flops 1610612736 | bytes 9175040 | tf_op jit(solution)/shard_map/dot_general | solution.py:77
  378.8 0.3 reshape.51
  379.1 1.0 fusion.4
  380.2 0.2 copy.27
  380.3 10.7 %all_to_all.17 = f32[4,64,512]{2,1,0:T(8,128)S(1)} all-to-all(f32[4,64,512]{2,1,0:T(8,128)S(1)} %bitcast.41), channel_id=1, replica_groups=mesh['gz_0'=8,'gz_1'=4,'gz_2'=2,'col'=4] {'col'}, dimensions={0} | all-to-all | bytes 1048576 | tf_op jit(solution)/shard_map/all_to_all | solution.py:42
  391.1 1.8 fusion.8
  (18 shorter events, 0.2 us)
Async XLA Ops:
  6.5 1.2 copy-start
  6.5 125.6 %reduce-scatter.8.cloned.1.call-start = ((), (), s32[]{:S(2)}) async-start(), calls=%async_computation.6 | async-start | bytes 9437184 | tf_op jit(solution)/shard_map/reduce_scatter | solution.py:30
  35.0 123.3 %copy-start.3 = (f32[512]{0:T(512)S(1)}, f32[512]{0:T(512)}, u32[]{:S(2)}) copy-start(f32[512]{0:T(512)} %param.13) | copy-start | bytes 6148
  35.0 124.1 %copy-start.4 = (f32[4]{0:T(128)S(1)}, f32[4]{0:T(128)}, u32[]{:S(2)}) copy-start(f32[4]{0:T(128)} %param.12) | copy-start | bytes 52
  35.0 123.3 %reduce-scatter.10.cloned.1.call-start = ((), (), s32[]{:S(2)}) async-start(), calls=%async_computation.7 | async-start | bytes 1310720
  134.7 41.2 %reduce-scatter.12.cloned.1.call-start = ((), (), s32[]{:S(2)}) async-start(), calls=%async_computation.8 | async-start | bytes 393216
  178.8 194.4 %copy-start.1 = (f32[64,1024]{1,0:T(8,128)S(1)}, f32[64,1024]{1,0:T(8,128)}, u32[]{:S(2)}) copy-start(f32[64,1024]{1,0:T(8,128)} %param.8) | copy-start | bytes 786436
  373.2 5.9 %copy-start.2 = (f32[4,4]{1,0:T(4,128)S(1)}, f32[4,4]{1,0:T(4,128)}, u32[]{:S(2)}) copy-start(f32[4,4]{1,0:T(4,128)} %param.9) | copy-start | bytes 196
Sparse Core Ops, SparseCore 0:
  35.2 96.9 reduce-scatter.7
  134.8 23.4 reduce-scatter.9
  160.8 15.0 reduce-scatter.11
